TPU v7x, 32 devices: a whole 2x2x4 slice. The times are simulated.
32 devices in a mesh: grp: 4 (over z), dev: 8 (over y, x, core).
Axes of the slice: x: 2, y: 2, z: 4, core: 2. Of those that a mesh axis runs over, the one named last changes fastest.
Arguments:
- a_blocks: bfloat16 [1024, 7, 192, 192], P(('grp', 'dev')), may hold values from -0.4375 to 0.4375
- prolong_t: bfloat16 [1024, 32, 192], P(('grp', 'dev')), may hold values from -1.796875 to 1.796875
- elem_slot: int32 [1024], P(('grp', 'dev')), may hold values from 0 to 5, as said below
- touch_agg: int32 [32, 6], replicated, may hold values from 0 to 135, as said below
- nbr: int32 [1024, 6], P(('grp', 'dev')), may hold values from -1 to 1023, as said below
- nbr_agg: int32 [1024, 6], P(('grp', 'dev')), may hold values from -1 to 135, as said below
- coarse_row: int32 [136], replicated, may hold values from 0 to 191, as said below
Outputs:
- coarse: float32 [192, 7, 1024], P('dev')
Inputs may be any that keep to these rules, and one draw needn't show every extreme that they name: Element e lies on device e // 32 (devices numbered grp-major). elem_slot[e] is the position of e's aggregate in touch_agg[e // 32]. `touch_agg`: each row lists 6 distinct aggregates, exactly those of the device's elements; all devices that touch one aggregate share their grp index. `nbr`: global element index across each face, or -1 on the domain's boundary; adjacency is symmetric; a neighbour lies on the same device, or on the device whose grp index differs by one (same dev index), or whose dev index differs by one (same grp index); exactly 8 elements of a device have a neighbour on each existing device next along grp, and exactly 8 on each existing device next along dev. `nbr_agg`: the aggregate of the element nbr[e, f], -1 exactly where nbr[e, f] is -1. Distinct values; aggregate a's row belongs to dev index coarse_row[a] // 24. Of the aggregates touched by one device at most 1 belong to one dev index, and of those touched by the devices of one grp index at most 6; one dev index reaches both bounds and holds 24 rows.
All inputs are finite; a program needn't handle non-finite values.
Results may differ from a plain program's by a relative error of at most 0.005.
Values may be sent and summed in bfloat16 or wider, within the bound.
A program may use at most 128 MiB of HBM per device.

v0:
```python
import jax
import jax.numpy as jnp
from jax import lax
from jax.sharding import PartitionSpec as P

EY = 4
TOUCH = 6


def extended(array, sides, width):
    for axis, dim in sides:
        size, length = (lax.axis_size(axis), array.shape[dim])
        up = [(i, (i + 1) % size) for i in range(size - 1)]
        down = [(j, i) for i, j in up]
        last = lax.slice_in_dim(array, length - width, length, axis=dim)
        first = lax.slice_in_dim(array, 0, width, axis=dim)
        before = lax.ppermute(last, axis, up)
        after = lax.ppermute(first, axis, down)
        array = jnp.concatenate([before, array, after], axis=dim)
    return array


def lookup_small(table, index):
    matches = index[..., None] == jnp.arange(table.shape[0], dtype=jnp.int32)
    return jnp.sum(jnp.where(matches, table, 0), axis=-1)


def owner_ranks(owners, width):
    tagged = (owners[..., :, None] == jnp.arange(width, dtype=jnp.int32)).astype(jnp.int32)
    earlier = jnp.cumsum(tagged, axis=-2) - tagged
    return jnp.sum(earlier * tagged, axis=-1)


def on_device(a_blocks, prolong_t, elem_slot, touch_agg, nbr, nbr_agg, coarse_row):
    n_grp = lax.axis_size("grp")
    n_dev = lax.axis_size("dev")
    grp_index = lax.axis_index("grp")
    dev_index = lax.axis_index("dev")
    device = grp_index * n_dev + dev_index
    e_dev, width_c, width_b = prolong_t.shape
    half_y = EY // 2
    span_y = half_y + 1
    box_rows = n_dev * half_y + 1
    send_cap = (TOUCH + n_dev - 1) // n_dev
    group_rows = send_cap * ((box_rows + half_y) // span_y)
    rows_own = n_grp * group_rows
    row_width = width_c * width_c
    touched = lax.dynamic_index_in_dim(touch_agg, device, 0, keepdims=False)
    own_agg = lookup_small(touched, elem_slot)
    left_blocks = jnp.einsum(
        "ecb,ekbd->ekcd", prolong_t, a_blocks, preferred_element_type=jnp.float32
    ).astype(jnp.bfloat16)
    valid = nbr >= 0
    safe_nbr = jnp.where(valid, nbr, device * e_dev)
    source = safe_nbr // e_dev
    local = safe_nbr % e_dev
    source_grp = source // n_dev
    source_dev = source % n_dev
    padded = extended(prolong_t[None, None], (("grp", 0), ("dev", 1)), 1)
    blocks_pool = padded.reshape(9 * e_dev, width_c, width_b)
    where_from = ((source_grp - grp_index + 1) * 3 + (source_dev - dev_index + 1)) * e_dev + local
    neighbours = jnp.take(blocks_pool, where_from, axis=0)
    right_blocks = jnp.concatenate([prolong_t[:, None], neighbours], axis=1)
    products = jnp.einsum(
        "ekcd,ekxd->ekcx", left_blocks, right_blocks, preferred_element_type=jnp.float32
    ).reshape(e_dev, 7, row_width)
    same = valid & (nbr_agg == own_agg[:, None])
    apart = valid & jnp.logical_not(same)
    faces = products[:, 1:]
    diagonal = products[:, 0] + jnp.sum(jnp.where(same[:, :, None], faces, 0.0), axis=1)
    contrib = jnp.concatenate([diagonal[:, None], jnp.where(apart[:, :, None], faces, 0.0)], axis=1)
    member = (elem_slot[None, :] == jnp.arange(TOUCH, dtype=jnp.int32)[:, None]).astype(jnp.float32)
    partial_rows = jnp.dot(
        member,
        contrib.reshape(e_dev, 7 * row_width),
        precision=lax.Precision.HIGHEST,
        preferred_element_type=jnp.float32,
    ).reshape(TOUCH, 7, row_width)
    target_rows = lookup_small(coarse_row, touched)
    group_touch = lax.dynamic_slice_in_dim(touch_agg, grp_index * n_dev, n_dev, 0)
    group_targets = lookup_small(coarse_row, group_touch)
    owners = target_rows // rows_own
    slots = owners * send_cap + owner_ranks(owners, n_dev)
    outgoing = jax.ops.segment_sum(partial_rows, slots, num_segments=n_dev * send_cap)
    incoming = lax.all_to_all(outgoing, "dev", split_axis=0, concat_axis=0, tiled=True)
    sender_owners = group_targets // rows_own
    sender_ranks = owner_ranks(sender_owners, n_dev)
    matched = (sender_owners == dev_index)[:, :, None] & (
        sender_ranks[:, :, None] == jnp.arange(send_cap, dtype=jnp.int32)[None, None, :]
    )
    places = jnp.sum(jnp.where(matched, (group_targets % rows_own)[:, :, None], 0), axis=1)
    places = places + rows_own * (1 - jnp.any(matched, axis=1).astype(jnp.int32))
    table = jax.ops.segment_sum(incoming, places.reshape(-1), num_segments=rows_own + 1)[:rows_own]
    all_targets = lookup_small(coarse_row, touch_agg).reshape(n_grp, n_dev * TOUCH)
    owned = all_targets // rows_own == dev_index
    present = jnp.any(
        owned[:, :, None]
        & ((all_targets % rows_own)[:, :, None] == jnp.arange(rows_own, dtype=jnp.int32)),
        axis=1,
    )
    ranking = jnp.cumsum(present.astype(jnp.int32), axis=1) - 1
    own_present = lax.dynamic_index_in_dim(present, grp_index, 0, keepdims=False)
    own_ranking = lax.dynamic_index_in_dim(ranking, grp_index, 0, keepdims=False)
    chosen = own_present[None, :] & (
        own_ranking[None, :] == jnp.arange(group_rows, dtype=jnp.int32)[:, None]
    )
    source_rows = jnp.sum(
        jnp.where(chosen, jnp.arange(rows_own, dtype=jnp.int32)[None, :], 0), axis=1
    )
    filled = jnp.any(chosen, axis=1)
    packed = jnp.where(filled[:, None, None], jnp.take(table, source_rows, axis=0), 0.0)
    home_group = jnp.sum(jnp.where(present, jnp.arange(n_grp, dtype=jnp.int32)[:, None], 0), axis=0)
    anywhere = jnp.any(present, axis=0)
    compact = home_group * group_rows + jnp.sum(jnp.where(present, ranking, 0), axis=0)
    piece = lax.all_gather(packed, "grp", axis=0, tiled=True)
    count = piece.shape[0]
    inside = anywhere & (compact >= 0) & (compact < count)
    arrived_rows = jnp.take(piece, jnp.clip(compact, 0, count - 1), axis=0)
    return jnp.where(inside[:, None, None], arrived_rows, 0.0)


def solution(mesh):
    in_specs = (
        P(("grp", "dev"), None, None, None),
        P(("grp", "dev"), None, None),
        P(("grp", "dev")),
        P(),
        P(("grp", "dev"), None),
        P(("grp", "dev"), None),
        P(),
    )
    out_specs = P("dev", None, None)
    return jax.shard_map(
        on_device, mesh=mesh, in_specs=in_specs, out_specs=out_specs, check_vma=False
    )
```

profile of v0, /device:TPU:0, one launch (start us, length us, event | category | flops | bytes accessed | tf_op | source)
XLA Modules:
  0.0 110.2 jit_solution(9970765389436165951)
XLA Ops:
  0.0 5.1 %collective-permute-start = (bf16[1,1,32,32,192]{4,3,2,1,0:T(8,128)(2,1)}, bf16[1,1,32,32,192]{4,3,2,1,0:T(8,128)(2,1)S(1)}, u32[]{:S(2)}, u32[]{:S(2)}) collective-permute-start(bf16[1,1,32,32,192]{4,3,2,1,0:T(8,128)(2,1)} %bitcast.64), channel_id=1, source_target_pairs={{0,8},{8,16},{16,24},{1,9},{9,17},{17,25},{2,10},{10,18},{18,26},{... | collective-permute-start | bytes 1179656 | tf_op jit(solution)/shard_map/ppermute | solution.py:17
  5.1 1.3 %collective-permute-start.1 = (bf16[1,1,32,32,192]{4,3,2,1,0:T(8,128)(2,1)}, bf16[1,1,32,32,192]{4,3,2,1,0:T(8,128)(2,1)S(1)}, u32[]{:S(2)}, u32[]{:S(2)}) collective-permute-start(bf16[1,1,32,32,192]{4,3,2,1,0:T(8,128)(2,1)} %bitcast.65), channel_id=1, source_target_pairs={{8,0},{16,8},{24,16},{9,1},{17,9},{25,17},{10,2},{18,10},{26,18},{... | collective-permute-start | bytes 1179656 | tf_op jit(solution)/shard_map/ppermute | solution.py:18
  6.4 1.0 select_reduce_fusion.1
  8.7 0.9 dynamic-slice_reduce_fusion
  9.5 0.9 select_reduce_fusion.3
  12.5 0.8 constant_dynamic-slice_fusion
  13.3 0.9 select_reduce_fusion.2
  14.6 2.0 %collective-permute-done = bf16[1,1,32,32,192]{4,3,2,1,0:T(8,128)(2,1)S(1)} collective-permute-done((bf16[1,1,32,32,192]{4,3,2,1,0:T(8,128)(2,1)}, bf16[1,1,32,32,192]{4,3,2,1,0:T(8,128)(2,1)S(1)}, u32[]{:S(2)}, u32[]{:S(2)}) %collective-permute-start) | collective-permute-done | bytes 393248 | tf_op jit(solution)/shard_map/ppermute | solution.py:17
  16.6 4.0 %collective-permute-done.1 = bf16[1,1,32,32,192]{4,3,2,1,0:T(8,128)(2,1)S(1)} collective-permute-done((bf16[1,1,32,32,192]{4,3,2,1,0:T(8,128)(2,1)}, bf16[1,1,32,32,192]{4,3,2,1,0:T(8,128)(2,1)S(1)}, u32[]{:S(2)}, u32[]{:S(2)}) %collective-permute-start.1) | collective-permute-done | bytes 393248 | tf_op jit(solution)/shard_map/ppermute | solution.py:18
  20.6 1.4 %pad_maximum_fusion.2 = bf16[3,1,32,32,192]{4,3,2,1,0:T(8,128)(2,1)S(1)} fusion(bf16[1,1,32,32,192]{4,3,2,1,0:T(8,128)(2,1)S(1)} %collective-permute-done.1, bf16[1,1,32,32,192]{4,3,2,1,0:T(8,128)(2,1)} %bitcast.66, bf16[1,1,32,32,192]{4,3,2,1,0:T(8,128)(2,1)S(1)} %collective-permute-done), kind=kLoop, calls=%fused_computation.12 | loop fusion | flops 1179648 | bytes 2359296 | tf_op jit(solution)/shard_map/concatenate | solution.py:19
  22.0 1.4 %collective-permute-start.2 = (bf16[3,1,32,32,192]{4,3,2,1,0:T(8,128)(2,1)S(1)}, bf16[3,1,32,32,192]{4,3,2,1,0:T(8,128)(2,1)S(1)}, u32[]{:S(2)}, u32[]{:S(2)}) collective-permute-start(bf16[3,1,32,32,192]{4,3,2,1,0:T(8,128)(2,1)S(1)} %pad_maximum_fusion.2), channel_id=1, source_target_pairs={{0,1},{1,2},{2,3},{3,4},{4,5},{5,6},{6,7},{8,9},{9,10},{10,11},{11... | collective-permute-start | bytes 3538952 | tf_op jit(solution)/shard_map/ppermute | solution.py:17
  23.4 1.3 %collective-permute-start.3 = (bf16[3,1,32,32,192]{4,3,2,1,0:T(8,128)(2,1)S(1)}, bf16[3,1,32,32,192]{4,3,2,1,0:T(8,128)(2,1)S(1)}, u32[]{:S(2)}, u32[]{:S(2)}) collective-permute-start(bf16[3,1,32,32,192]{4,3,2,1,0:T(8,128)(2,1)S(1)} %pad_maximum_fusion.2), channel_id=1, source_target_pairs={{1,0},{2,1},{3,2},{4,3},{5,4},{6,5},{7,6},{9,8},{10,9},{11,10},{12... | collective-permute-start | bytes 3538952 | tf_op jit(solution)/shard_map/ppermute | solution.py:18
  24.7 13.3 %convolution_convert_fusion = bf16[32,7,192,32]{2,3,1,0:T(8,128)(2,1)} fusion(bf16[32,7,192,192]{3,2,1,0:T(8,128)(2,1)} %param.7, bf16[32,32,192]{2,1,0:T(8,128)(2,1)S(1)} %copy-done.1), kind=kOutput, calls=%fused_computation.11 | convolution fusion | flops 529858560 | bytes 19660800 | tf_op jit(solution)/shard_map/ecb,ekbd->ekcd/dot_general | solution.py:50
  38.0 2.8 %pad_maximum_fusion = bf16[3,3,32,32,192]{4,3,2,1,0:T(8,128)(2,1)} fusion(bf16[3,1,32,32,192]{4,3,2,1,0:T(8,128)(2,1)S(1)} %collective-permute-done.3, bf16[1,1,32,32,192]{4,3,2,1,0:T(8,128)(2,1)S(1)} %collective-permute-done.1, bf16[1,1,32,32,192]{4,3,2,1,0:T(8,128)(2,1)S(1)} %bitcast.67, bf16[1,1,32,32,192]{4,3,2,1,0:T(8,128)(2,1)S(1)} %collective-permute-done, ...), kind=kLoop, calls=%fused_computation.5 | loop fusion | flops 7077888 | bytes 7077888 | tf_op jit(solution)/shard_map/concatenate | solution.py:19
  40.9 3.2 %gather_fusion = bf16[192,32,192]{2,1,0:T(8,128)(2,1)S(1)} fusion(bf16[288,32,192]{2,1,0:T(8,128)(2,1)} %bitcast.62, s32[1024]{0:T(1024)S(1)} %pad_clamp_fusion.2), kind=kCustom, calls=%fused_computation | custom fusion | bytes 4719360 | tf_op jit(solution)/shard_map/jit(_take)/gather | solution.py:62
  44.6 1.5 %copy-done = bf16[32,7,192,32]{2,3,1,0:T(8,128)(2,1)S(1)} copy-done((bf16[32,7,192,32]{2,3,1,0:T(8,128)(2,1)S(1)}, bf16[32,7,192,32]{2,3,1,0:T(8,128)(2,1)}, u32[]{:S(2)}) %copy-start) | copy-done | bytes 2752536
  46.2 2.5 %fusion = f32[32,7,32,32]{3,2,0,1:T(8,128)} fusion(bf16[32,7,192,32]{2,3,1,0:T(8,128)(2,1)S(1)} %copy-done, bf16[32,6,32,192]{3,2,1,0:T(8,128)(2,1)S(1)} %broadcast_select_fusion, bf16[32,1,32,192]{3,2,1,0:T(8,128)(2,1)S(1)} %bitcast.68), kind=kOutput, calls=%fused_computation.7 | convolution fusion | flops 89456640 | bytes 6422528 | tf_op jit(solution)/shard_map/ekcd,ekxd->ekcx/dot_general | solution.py:64
  48.7 3.3 %reshape.226 = f32[32,7,1024]{2,0,1:T(8,128)S(1)} reshape(f32[32,7,32,32]{3,2,0,1:T(8,128)} %fusion) | data formatting | bytes 1835008 | tf_op jit(solution)/shard_map/reshape | solution.py:66
  53.5 2.2 %scatter_fusion = f32[8,7,1024]{2,1,0:T(8,128)} fusion(f32[8,7,1024]{2,1,0:T(8,128)} %broadcast_in_dim.193, s32[6]{0:T(128)S(1)} %fusion.41, f32[6,7,1024]{2,1,0:T(8,128)S(1)} %copy.47), kind=kCustom, calls=%fused_computation.3 | custom fusion | flops 43008 | bytes 516120 | tf_op jit(solution)/shard_map/scatter-add | solution.py:84
  55.7 25.7 %all-to-all-start = ((f32[8,7,1024]{2,1,0:T(8,128)}), f32[8,7,1024]{2,1,0:T(8,128)S(1)}, u32[]{:S(2)}, u32[]{:S(2)}) async-start(f32[8,7,1024]{2,1,0:T(8,128)} %scatter_fusion), calls=%async_computation | async-start | bytes 524288 | tf_op jit(solution)/shard_map/all_to_all | solution.py:85
  81.4 6.9 %all-to-all-done = f32[8,7,1024]{2,1,0:T(8,128)S(1)} async-done(((f32[8,7,1024]{2,1,0:T(8,128)}), f32[8,7,1024]{2,1,0:T(8,128)S(1)}, u32[]{:S(2)}, u32[]{:S(2)}) %all-to-all-start) | async-done | bytes 229408 | tf_op jit(solution)/shard_map/all_to_all | solution.py:85
  88.4 0.9 scatter_fusion.1
  90.1 18.1 %all_gather.3 = f32[24,7,1024]{2,1,0:T(8,128)S(1)} all-gather(f32[6,7,1024]{2,1,0:T(8,128)S(1)} %select_select_fusion.1), channel_id=1, replica_groups=mesh['grp'=4,'dev'=8] {'grp'}, dimensions={0}, use_global_device_ids=true | all-gather | bytes 860160 | tf_op jit(solution)/shard_map/all_gather | solution.py:115
  108.9 1.2 %copy.48 = f32[24,7,1024]{2,0,1:T(8,128)} copy(f32[24,7,1024]{2,1,0:T(8,128)S(1)} %select_select_fusion) | data formatting | bytes 1376256 | tf_op jit(solution)/shard_map/jit(_where)/select_n | solution.py:119
  (61 shorter events, 7.3 us)
Async XLA Ops:
  0.0 24.7 %copy-start.1 = (bf16[32,32,192]{2,1,0:T(8,128)(2,1)S(1)}, bf16[32,32,192]{2,1,0:T(8,128)(2,1)}, u32[]{:S(2)}) copy-start(bf16[32,32,192]{2,1,0:T(8,128)(2,1)} %param.8) | copy-start | bytes 1179652
  0.0 16.6 %collective-permute-start = (bf16[1,1,32,32,192]{4,3,2,1,0:T(8,128)(2,1)}, bf16[1,1,32,32,192]{4,3,2,1,0:T(8,128)(2,1)S(1)}, u32[]{:S(2)}, u32[]{:S(2)}) collective-permute-start(bf16[1,1,32,32,192]{4,3,2,1,0:T(8,128)(2,1)} %bitcast.64), channel_id=1, source_target_pairs={{0,8},{8,16},{16,24},{1,9},{9,17},{17,25},{2,10},{10,18},{18,26},{... | collective-permute-start | bytes 1179656 | tf_op jit(solution)/shard_map/ppermute | solution.py:17
  5.1 15.5 %collective-permute-start.1 = (bf16[1,1,32,32,192]{4,3,2,1,0:T(8,128)(2,1)}, bf16[1,1,32,32,192]{4,3,2,1,0:T(8,128)(2,1)S(1)}, u32[]{:S(2)}, u32[]{:S(2)}) collective-permute-start(bf16[1,1,32,32,192]{4,3,2,1,0:T(8,128)(2,1)} %bitcast.65), channel_id=1, source_target_pairs={{8,0},{16,8},{24,16},{9,1},{17,9},{25,17},{10,2},{18,10},{26,18},{... | collective-permute-start | bytes 1179656 | tf_op jit(solution)/shard_map/ppermute | solution.py:18
  22.0 16.0 %collective-permute-start.2 = (bf16[3,1,32,32,192]{4,3,2,1,0:T(8,128)(2,1)S(1)}, bf16[3,1,32,32,192]{4,3,2,1,0:T(8,128)(2,1)S(1)}, u32[]{:S(2)}, u32[]{:S(2)}) collective-permute-start(bf16[3,1,32,32,192]{4,3,2,1,0:T(8,128)(2,1)S(1)} %pad_maximum_fusion.2), channel_id=1, source_target_pairs={{0,1},{1,2},{2,3},{3,4},{4,5},{5,6},{6,7},{8,9},{9,10},{10,11},{11... | collective-permute-start | bytes 3538952 | tf_op jit(solution)/shard_map/ppermute | solution.py:17
  23.4 14.6 %collective-permute-start.3 = (bf16[3,1,32,32,192]{4,3,2,1,0:T(8,128)(2,1)S(1)}, bf16[3,1,32,32,192]{4,3,2,1,0:T(8,128)(2,1)S(1)}, u32[]{:S(2)}, u32[]{:S(2)}) collective-permute-start(bf16[3,1,32,32,192]{4,3,2,1,0:T(8,128)(2,1)S(1)} %pad_maximum_fusion.2), channel_id=1, source_target_pairs={{1,0},{2,1},{3,2},{4,3},{5,4},{6,5},{7,6},{9,8},{10,9},{11,10},{12... | collective-permute-start | bytes 3538952 | tf_op jit(solution)/shard_map/ppermute | solution.py:18
  44.1 2.0 %copy-start = (bf16[32,7,192,32]{2,3,1,0:T(8,128)(2,1)S(1)}, bf16[32,7,192,32]{2,3,1,0:T(8,128)(2,1)}, u32[]{:S(2)}) copy-start(bf16[32,7,192,32]{2,3,1,0:T(8,128)(2,1)} %convolution_convert_fusion) | copy-start | bytes 8257540
  44.1 2.1 %copy-start.2 = (bf16[32,32,192]{2,1,0:T(8,128)(2,1)S(1)}, bf16[32,32,192]{2,1,0:T(8,128)(2,1)}, u32[]{:S(2)}) copy-start(bf16[32,32,192]{2,1,0:T(8,128)(2,1)} %param.8) | copy-start | bytes 1179652
  48.7 3.6 %copy-start.3 = (s32[32]{0:T(128)S(1)}, s32[32]{0:T(128)}, u32[]{:S(2)}) copy-start(s32[32]{0:T(128)} %param.9) | copy-start | bytes 388
  55.7 32.6 %all-to-all-start = ((f32[8,7,1024]{2,1,0:T(8,128)}), f32[8,7,1024]{2,1,0:T(8,128)S(1)}, u32[]{:S(2)}, u32[]{:S(2)}) async-start(f32[8,7,1024]{2,1,0:T(8,128)} %scatter_fusion), calls=%async_computation | async-start | bytes 524288 | tf_op jit(solution)/shard_map/all_to_all | solution.py:85
where the time goes:
time: 111 us; the launch traced here: 110 us
  starting transfers between devices  34.8 us (31%)
  blocking collectives  18.1 us (16%)
  matrix products  16.2 us (15%)
  local copies, waits for them, and re-layouts  14.1 us (13%)
  other arithmetic  13.8 us (12%)
  waiting for transfers between devices  12.9 us (12%)
    all_to_all x1, starting transfers between devices, on_device(): lax.all_to_all(outgoing, 'dev', split_axis=0, concat_axis=0, tiled=True)  25.7 us
    all_gather x1, blocking collectives, on_device(): piece = lax.all_gather(packed, 'grp', axis=0, tiled=True)  18.1 us
    dot_general x1, matrix products, on_device(): jnp.einsum('ecb,ekbd->ekcd', prolong_t, a_blocks, preferred_element_type=...  13.3 us
    all_to_all x1, waiting for transfers between devices, on_device(): lax.all_to_all(outgoing, 'dev', split_axis=0, concat_axis=0, tiled=True)  6.89 us
    ppermute x2, starting transfers between devices, extended(): before = lax.ppermute(last, axis, up)  6.5 us
    concatenate x2, other arithmetic, extended(): array = jnp.concatenate([before, array, after], axis=dim)  4.21 us
    ppermute x2, waiting for transfers between devices, extended(): after = lax.ppermute(first, axis, down)  4.04 us
    reduce_sum x4, other arithmetic, lookup_small(): return jnp.sum(jnp.where(matches, table, 0), axis=-1)  3.48 us
  transfers between devices with their start and end apart: 5, of which 3 were waited for; matrix products, arithmetic and copies ran while one was open for 19% of the time, Pallas kernels for 0%

commit v1 on v0

v1 whole, which is shorter than its diff:
```python
import functools

import jax
import jax.numpy as jnp
from jax import lax
from jax.experimental import pallas as pl
from jax.experimental.pallas import tpu as pltpu
from jax.sharding import PartitionSpec as P

EX = 4
EY = 4
MESH = pl.DeviceIdType.MESH
F32 = jnp.float32
BF16 = jnp.bfloat16


def iota(shape, dim):
    return lax.broadcasted_iota(jnp.int32, shape, dim)


def kernel(
    n_grp, n_dev, halo, group_rows,
    sidx, wf, slot, tinv, pos, cidx,
    a_ref, p_ref, ms_ref, ma_ref,
    out_ref,
    a_buf, pool, pack, left, prod_s, prod_a, part_t, parts, inbox, gathered, flat,
    a_sem, h_send, h_recv, x_send, x_recv, g_send, g_recv,
):
    grp = lax.axis_index("grp")
    dev = lax.axis_index("dev")
    e_dev, width_c, width_b = p_ref.shape
    n_k = a_ref.shape[1]
    touch = part_t.shape[0] - 1
    rows_own = out_ref.shape[0]
    wide = n_k * width_c
    lane = 128
    rep = lane // width_c
    sub = width_c // rep

    def a_copy(e):
        return pltpu.make_async_copy(a_ref.at[e], a_buf.at[e], a_sem.at[e])

    @pl.loop(0, e_dev)
    def _(e):
        a_copy(e).start()

    barrier = pltpu.get_barrier_semaphore()
    for off in range(1, n_dev):
        pl.semaphore_signal(
            barrier, inc=1, device_id=(grp, lax.rem(dev + off, n_dev)), device_id_type=MESH
        )
    for off in range(1, n_grp):
        pl.semaphore_signal(
            barrier, inc=1, device_id=(lax.rem(grp + off, n_grp), dev), device_id_type=MESH
        )

    for j in range(4 * halo):
        pack[j] = p_ref[sidx[j]]
    pool[0:e_dev] = p_ref[...]
    pl.semaphore_wait(barrier, n_dev + n_grp - 2)

    dirs = (
        (grp > 0, (grp - 1, dev)),
        (grp < n_grp - 1, (grp + 1, dev)),
        (dev > 0, (grp, dev - 1)),
        (dev < n_dev - 1, (grp, dev + 1)),
    )

    def halo_copy(d, target):
        back = d ^ 1
        return pltpu.make_async_remote_copy(
            src_ref=pack.at[pl.ds(d * halo, halo)],
            dst_ref=pool.at[pl.ds(e_dev + back * halo, halo)],
            send_sem=h_send.at[d],
            recv_sem=h_recv.at[back],
            device_id=target,
            device_id_type=MESH,
        )

    for d, (there, target) in enumerate(dirs):
        @pl.when(there)
        def _(d=d, target=target):
            halo_copy(d, target).start()

    @pl.loop(0, e_dev)
    def _(e):
        a_copy(e).wait()
        own = p_ref[e]
        for k in range(n_k):
            left[e, k * width_c:(k + 1) * width_c, :] = jnp.dot(
                own, a_buf[e, k], preferred_element_type=F32
            ).astype(BF16)

    for d, (there, target) in enumerate(dirs):
        @pl.when(there)
        def _(d=d, target=target):
            halo_copy(d, target).wait_send()
            pltpu.make_async_remote_copy(
                src_ref=pack.at[pl.ds(d * halo, halo)],
                dst_ref=pool.at[pl.ds(e_dev + d * halo, halo)],
                send_sem=h_send.at[d],
                recv_sem=h_recv.at[d],
                device_id=target,
                device_id_type=MESH,
            ).wait_recv()

    group_of_lane = iota((width_c, wide), 1) // width_c

    @pl.loop(0, e_dev)
    def _(e):
        right = jnp.concatenate(
            [pool[e]] + [pool[wf[e * (n_k - 1) + f]] for f in range(n_k - 1)], axis=0
        )
        full = lax.dot_general(
            left[e], right, (((1,), (1,)), ((), ())), preferred_element_type=F32
        )
        picked = full[0:width_c]
        for k in range(1, n_k):
            picked = jnp.where(group_of_lane == k, full[k * width_c:(k + 1) * width_c], picked)
        prod_s[e] = jnp.where(ms_ref[pl.ds(e, 1), :] > 0, picked, 0.0)
        prod_a[e] = jnp.where(ma_ref[pl.ds(e, 1), :] > 0, picked, 0.0)

    spread_s = (iota((wide, lane), 0) % width_c == iota((wide, lane), 1) % width_c).astype(F32).astype(BF16)
    rest = (n_k - 1) * lane
    spread_a = (
        iota((wide, rest), 0)
        == (iota((wide, rest), 1) // lane + 1) * width_c + iota((wide, rest), 1) % width_c
    ).astype(F32).astype(BF16)
    keep = iota((width_c, n_k * lane), 0) % rep == (iota((width_c, n_k * lane), 1) % lane) // width_c
    squeeze = (iota((sub, width_c), 1) // rep == iota((sub, width_c), 0)).astype(F32).astype(BF16)

    part_t[touch] = jnp.zeros(part_t.shape[1:], BF16)

    def spread(value, table):
        high = value.astype(BF16)
        low = (value - high.astype(F32)).astype(BF16)
        return jnp.dot(high, table, preferred_element_type=F32) + jnp.dot(
            low, table, preferred_element_type=F32
        )

    for t in range(touch):
        zero = jnp.zeros((width_c, wide), F32)

        def add(e, sums, t=t):
            sum_s, sum_a = sums
            member = jnp.where(slot[e] == t, 1.0, 0.0).astype(F32)
            return sum_s + prod_s[e] * member, sum_a + prod_a[e] * member

        sum_s, sum_a = lax.fori_loop(0, e_dev, add, (zero, zero), unroll=4)
        both = jnp.concatenate([spread(sum_s, spread_s), spread(sum_a, spread_a)], axis=1)
        both = jnp.where(keep, both, 0.0).astype(BF16)
        rows = jnp.dot(squeeze, both, preferred_element_type=F32)
        rows = jnp.concatenate([rows[:, s * lane:(s + 1) * lane] for s in range(n_k)], axis=0)
        part_t[t] = rows.astype(BF16)

    for o in range(n_dev):
        parts[o] = part_t[tinv[o]]
    inbox[dev] = parts[dev]

    def part_copy(off):
        target = lax.rem(dev + off, n_dev)
        return pltpu.make_async_remote_copy(
            src_ref=parts.at[target],
            dst_ref=inbox.at[dev],
            send_sem=x_send.at[off],
            recv_sem=x_recv.at[off],
            device_id=(grp, target),
            device_id_type=MESH,
        )

    def part_arrival(off):
        sender = lax.rem(dev + n_dev - off, n_dev)
        return pltpu.make_async_remote_copy(
            src_ref=parts.at[sender],
            dst_ref=inbox.at[sender],
            send_sem=x_send.at[off],
            recv_sem=x_recv.at[off],
            device_id=(grp, sender),
            device_id_type=MESH,
        )

    for off in range(1, n_dev):
        part_copy(off).start()
    for off in range(1, n_dev):
        part_arrival(off).wait_recv()

    for j in range(group_rows):
        total = jnp.zeros(parts.shape[1:], F32)
        for d in range(n_dev):
            member = jnp.where(pos[d] == j, 1.0, 0.0).astype(F32)
            total = total + inbox[d].astype(F32) * member
        gathered[grp, j] = total.astype(BF16)

    def row_copy(off):
        target = lax.rem(grp + off, n_grp)
        return pltpu.make_async_remote_copy(
            src_ref=gathered.at[grp],
            dst_ref=gathered.at[grp],
            send_sem=g_send.at[off],
            recv_sem=g_recv.at[off],
            device_id=(target, dev),
            device_id_type=MESH,
        )

    def row_arrival(off):
        sender = lax.rem(grp + n_grp - off, n_grp)
        return pltpu.make_async_remote_copy(
            src_ref=gathered.at[sender],
            dst_ref=gathered.at[sender],
            send_sem=g_send.at[off],
            recv_sem=g_recv.at[off],
            device_id=(sender, dev),
            device_id_type=MESH,
        )

    for off in range(1, n_grp):
        row_copy(off).start()
    for off in range(1, n_grp):
        row_arrival(off).wait_recv()

    @pl.loop(0, rows_own)
    def _(r):
        at = cidx[r]
        safe = jnp.maximum(at, 0)
        row = gathered[safe // group_rows, safe % group_rows].astype(F32)
        flat[r] = jnp.where(at >= 0, row, 0.0)
        for j in range(sub):
            out_ref[r, :, j * lane:(j + 1) * lane] = flat[r, pl.ds(j, n_k, stride=sub), :]

    for off in range(1, n_dev):
        part_copy(off).wait_send()
    for off in range(1, n_grp):
        row_copy(off).wait_send()


def on_device(n_grp, n_dev, a_blocks, prolong_t, elem_slot, touch_agg, nbr, nbr_agg, coarse_row):
    grp = lax.axis_index("grp")
    dev = lax.axis_index("dev")
    device = grp * n_dev + dev
    e_dev, width_c, width_b = prolong_t.shape
    n_k = a_blocks.shape[1]
    touch = touch_agg.shape[1]
    halo = e_dev // EX
    half_y = EY // 2
    span_y = half_y + 1
    group_rows = (n_dev * half_y + 1 + half_y) // span_y
    rows_own = n_grp * group_rows
    assert touch <= n_dev
    i32 = jnp.int32

    def ar(n):
        return jnp.arange(n, dtype=i32)

    none = jnp.int32(-2)
    near = jnp.stack([
        jnp.where(grp > 0, device - n_dev, none),
        jnp.where(grp < n_grp - 1, device + n_dev, none),
        jnp.where(dev > 0, device - 1, none),
        jnp.where(dev < n_dev - 1, device + 1, none),
    ])
    source = jnp.where(nbr >= 0, nbr // e_dev, -1)
    local = nbr - source * e_dev
    hit = jnp.any(source[None] == near[:, None, None], axis=2).astype(i32)
    rank = jnp.sum(hit[:, None, :] * (ar(e_dev)[None, :] < ar(e_dev)[:, None]), axis=2)
    sidx = jnp.sum(
        jnp.where((rank[:, None, :] == ar(halo)[:, None]) & (hit[:, None, :] > 0), ar(e_dev), 0), axis=2
    ).reshape(-1)
    seen = jnp.any(
        nbr[None, None] == (near[:, None] * e_dev + ar(e_dev))[:, :, None, None], axis=(2, 3)
    ).astype(i32)
    behind = jnp.sum(
        jnp.where(
            source[:, :, None, None] == near[:, None],
            seen * (ar(e_dev) < local[:, :, None, None])
            + jnp.where(ar(e_dev) == 0, (e_dev + ar(4) * halo)[:, None], 0),
            0,
        ),
        axis=(2, 3),
    )
    wf = jnp.where(source == device, local, behind).reshape(-1)

    touched = lax.dynamic_index_in_dim(touch_agg, device, 0, keepdims=False)
    own_agg = jnp.sum(jnp.where(elem_slot[:, None] == ar(touch), touched, 0), axis=1)
    valid = nbr >= 0
    same = valid & (nbr_agg == own_agg[:, None])
    apart = valid & jnp.logical_not(same)
    true = jnp.ones((e_dev, 1), bool)
    ms = jnp.repeat(jnp.concatenate([true, same], axis=1).astype(F32), width_c, axis=1)
    ma = jnp.repeat(jnp.concatenate([~true, apart], axis=1).astype(F32), width_c, axis=1)

    targets = jnp.sum(
        jnp.where(touch_agg[:, :, None] == ar(coarse_row.shape[0]), coarse_row, 0), axis=2
    )
    owners = targets // rows_own
    mine = owners == dev
    place = jnp.where(mine, targets - owners * rows_own, -1)
    present = jnp.any(
        place.reshape(n_grp, n_dev * touch)[:, :, None] == ar(rows_own), axis=1
    ).astype(i32)
    cidx = jnp.sum(
        present[:, :, None]
        * (
            present[:, None, :] * (ar(rows_own)[None, :] < ar(rows_own)[:, None])
            + jnp.where(ar(rows_own) == 0, ar(n_grp)[:, None] * group_rows + 1, 0)[:, None, :]
        ),
        axis=(0, 2),
    ) - 1
    own_present = lax.dynamic_index_in_dim(present, grp, 0, keepdims=False)
    group_place = lax.dynamic_slice_in_dim(place, grp * n_dev, n_dev, 0)
    pos = jnp.sum(
        jnp.where(
            group_place[:, :, None] >= 0,
            own_present * (ar(rows_own) < group_place[:, :, None]) + (ar(rows_own) == 0),
            0,
        ),
        axis=(1, 2),
    ) - 1
    own_owner = lax.dynamic_index_in_dim(owners, device, 0, keepdims=False)
    tinv = touch + jnp.sum(
        jnp.where(own_owner[None, :] == ar(n_dev)[:, None], ar(touch) - touch, 0), axis=1
    )

    lane = 128
    flat_rows = n_k * width_c * width_c // lane
    smem = pl.BlockSpec(memory_space=pltpu.SMEM)
    vmem = pl.BlockSpec(memory_space=pltpu.VMEM)
    wide = n_k * width_c
    return pl.pallas_call(
        functools.partial(kernel, n_grp, n_dev, halo, group_rows),
        out_shape=jax.ShapeDtypeStruct((rows_own, n_k, width_c * width_c), F32),
        in_specs=[smem] * 6 + [pl.BlockSpec(memory_space=pl.ANY)] + [vmem] * 3,
        out_specs=vmem,
        scratch_shapes=[
            pltpu.VMEM(a_blocks.shape, BF16),
            pltpu.VMEM((e_dev + 4 * halo, width_c, width_b), BF16),
            pltpu.VMEM((4 * halo, width_c, width_b), BF16),
            pltpu.VMEM((e_dev, wide, width_b), BF16),
            pltpu.VMEM((e_dev, width_c, wide), F32),
            pltpu.VMEM((e_dev, width_c, wide), F32),
            pltpu.VMEM((touch + 1, flat_rows, lane), BF16),
            pltpu.VMEM((n_dev, flat_rows, lane), BF16),
            pltpu.VMEM((n_dev, flat_rows, lane), BF16),
            pltpu.VMEM((n_grp, group_rows, flat_rows, lane), BF16),
            pltpu.VMEM((rows_own, flat_rows, lane), F32),
            pltpu.SemaphoreType.DMA((e_dev,)),
            pltpu.SemaphoreType.DMA((4,)),
            pltpu.SemaphoreType.DMA((4,)),
            pltpu.SemaphoreType.DMA((n_dev,)),
            pltpu.SemaphoreType.DMA((n_dev,)),
            pltpu.SemaphoreType.DMA((n_grp,)),
            pltpu.SemaphoreType.DMA((n_grp,)),
        ],
        compiler_params=pltpu.CompilerParams(
            collective_id=0, has_side_effects=True, vmem_limit_bytes=60 * 1024 * 1024
        ),
        name="galerkin",
    )(sidx, wf, elem_slot, tinv, pos, cidx, a_blocks, prolong_t, ms, ma)


def solution(mesh):
    in_specs = (
        P(("grp", "dev"), None, None, None),
        P(("grp", "dev"), None, None),
        P(("grp", "dev")),
        P(),
        P(("grp", "dev"), None),
        P(("grp", "dev"), None),
        P(),
    )
    out_specs = P("dev", None, None)
    return jax.shard_map(
        functools.partial(on_device, mesh.shape["grp"], mesh.shape["dev"]),
        mesh=mesh, in_specs=in_specs, out_specs=out_specs, check_vma=False,
    )
```

time: 111 us -> 54.5 us (0.49)
  Pallas kernels: 0 us -> 39 us
  starting transfers between devices: 34.8 us -> 0 us
  blocking collectives: 18.1 us -> 0 us
  matrix products: 16.2 us -> 0 us
  waiting for transfers between devices: 12.9 us -> 0 us
  local copies, waits for them, and re-layouts: 14.1 us -> 6.65 us
  other arithmetic: 13.8 us -> 8.35 us
    pallas_call x0 -> x1, Pallas kernels: none -> 39 us  [on_device(): pl.pallas_call(functools.partial(kernel, n_grp, n_dev, halo, group_rows),...]
    all_to_all x1 -> x0, starting transfers between devices: 25.7 us -> none  [on_device(): lax.all_to_all(outgoing, 'dev', split_axis=0, concat_axis=0, tiled=True)]
    all_gather x1 -> x0, blocking collectives: 18.1 us -> none  [on_device(): piece = lax.all_gather(packed, 'grp', axis=0, tiled=True)]
    dot_general x3 -> x0, matrix products: 16.2 us -> none  [the longest x1 13.3 us: on_device(): jnp.einsum('ecb,ekbd->ekcd', prolong_t, a_blocks, preferred_element_type=...]
    ppermute x4 -> x0, starting transfers between devices: 9.08 us -> none  [the longest x2 6.5 us: extended(): before = lax.ppermute(last, axis, up)]
    all_to_all x1 -> x0, waiting for transfers between devices: 6.89 us -> none  [on_device(): lax.all_to_all(outgoing, 'dev', split_axis=0, concat_axis=0, tiled=True)]
    ppermute x4 -> x0, waiting for transfers between devices: 6 us -> none  [the longest x2 4.04 us: extended(): after = lax.ppermute(first, axis, down)]
    gather x3 -> x0, local copies, waits for them, and re-layouts: 4.38 us -> none  [the longest x1 3.22 us: on_device(): neighbours = jnp.take(blocks_pool, where_from, axis=0)]
  transfers between devices with their start and end apart: 5 -> 0, of which waited for: 3 -> 0; matrix products, arithmetic and copies ran while one was open for 19% -> 0% of each run, Pallas kernels for 0% -> 0%
where the time goes in v1:
time: 54.5 us; the launch traced here: 54.1 us
  Pallas kernels  39 us (72%)
  other arithmetic  8.35 us (15%)
  local copies, waits for them, and re-layouts  6.65 us (12%)
    pallas_call x1, Pallas kernels, on_device(): pl.pallas_call(functools.partial(kernel, n_grp, n_dev, halo, group_rows),...  39 us
    pallas_call x1, local copies, waits for them, and re-layouts, on_device(): pl.pallas_call(functools.partial(kernel, n_grp, n_dev, halo, group_rows),...  2.38 us

profile of v1, /device:TPU:0, one launch (start us, length us, event | category | flops | bytes accessed | tf_op | source)
XLA Modules:
  0.0 54.1 jit_solution(11491280876504250750)
XLA Ops:
  0.3 0.9 %compare_reduce_fusion = pred[4,32]{1,0:T(4,128)(4,1)S(1)} fusion(s32[4,32]{1,0:T(4,128)S(1)} %iota_add_fusion, s32[32,6]{0,1:T(8,128)} %param.11), kind=kLoop, calls=%fused_computation.1 | loop fusion | flops 49024 | bytes 1408 | tf_op jit(solution)/shard_map/reduce_or | solution.py:268
  1.3 1.0 %select_reduce_fusion.1 = s32[32,6]{0,1:T(8,128)S(1)} fusion(s32[136]{0:T(256)} %param.13, s32[32,6]{0,1:T(8,128)} %param.10), kind=kLoop, calls=%fused_computation.2 | loop fusion | flops 78144 | bytes 2080 | tf_op jit(solution)/shard_map/reduce_sum | solution.py:291
  2.3 0.9 %dynamic-slice_reduce_fusion = (s32[6]{0:T(128)S(1)}, s32[6]{0:T(128)S(1)}) fusion(s32[32,6]{0,1:T(8,128)} %param.10, s32[]{:T(128)S(6)} %select_n.107, s32[32,6]{0,1:T(8,128)S(1)} %get-tuple-element.12), kind=kLoop, calls=%fused_computation.29 | loop fusion | bytes 100 | tf_op jit(solution)/shard_map/jit(dynamic_index_in_dim)/dynamic_slice | solution.py:282
  3.2 0.7 %select_reduce_fusion.4 = s32[32]{0:T(128)S(1)} fusion(s32[6]{0:T(128)S(1)} %get-tuple-element.19, s32[32]{0:T(128)} %slot.1), kind=kLoop, calls=%fused_computation.28 | loop fusion | flops 544 | bytes 280 | tf_op jit(solution)/shard_map/reduce_sum | solution.py:283
  4.1 0.5 broadcast_add_fusion.2.tinv
  4.6 0.7 %not_and_fusion = (pred[32,6]{0,1:T(8,128)(4,1)S(1)}, pred[32,6]{0,1:T(8,128)(4,1)S(1)}) fusion(s32[32,6]{0,1:T(8,128)} %param.11, s32[32,6]{0,1:T(8,128)} %param.12, s32[32]{0:T(128)S(1)} %select_reduce_fusion.4), kind=kLoop, calls=%fused_computation.42 | loop fusion | flops 960 | bytes 2048 | tf_op jit(solution)/shard_map/and | solution.py:286
  5.3 0.7 %multiply_subtract_fusion = (s32[32,6]{0,1:T(8,128)S(1)}, s32[32,6]{0,1:T(8,128)S(1)}) fusion(s32[32,6]{0,1:T(8,128)} %param.11), kind=kLoop, calls=%fused_computation.37 | loop fusion | flops 3648 | bytes 2304 | tf_op jit(solution)/shard_map/sub | solution.py:262
  6.6 0.1 fusion.1
  6.8 0.2 select_reduce_fusion.2
  6.9 0.6 %broadcast_add_fusion.1.pos = s32[8]{0:T(128)} fusion(s32[8]{0:T(128)S(1)} %select_reduce_fusion.2), kind=kLoop, calls=%fused_computation.67 | loop fusion | flops 8 | bytes 64 | tf_op jit(solution)/shard_map/sub | solution.py:310
  7.5 0.2 multiply_reduce_fusion.1
  7.7 0.5 broadcast_add_fusion.cidx
  8.2 0.1 multiply_reduce_fusion
  8.4 0.2 select_reduce_fusion.3
  8.5 0.7 %reshape.227.sidx = s32[32]{0:T(128)} reshape(s32[4,8]{1,0:T(4,128)S(1)} %select_reduce_fusion.3) | data formatting | bytes 256 | tf_op jit(solution)/shard_map/reshape | solution.py:267
  9.2 0.1 fusion
  9.3 0.3 select_reduce_fusion
  9.6 0.7 %compare_select_fusion = s32[32,6]{0,1:T(8,128)S(1)} fusion(s32[32,6]{0,1:T(8,128)S(1)} %select_reduce_fusion, s32[]{:T(128)S(6)} %add.91, s32[32,6]{0,1:T(8,128)} %param.11), kind=kLoop, calls=%fused_computation.45 | loop fusion | flops 4032 | bytes 2308 | tf_op jit(solution)/shard_map/jit(_where)/select_n | solution.py:280
  10.3 0.1 copy.35
  10.4 0.7 %reshape.228.wf = s32[192]{0:T(256)} reshape(s32[32,6]{1,0:T(8,128)S(1)} %copy.35) | data formatting | bytes 1536 | tf_op jit(solution)/shard_map/reshape | solution.py:280
  11.2 0.7 %reshape.230.ma_ref = f32[32,224]{1,0:T(8,128)} reshape(f32[32,7,32]{2,1,0:T(8,128)S(1)} %broadcast_in_dim.146) | data formatting | bytes 57344 | tf_op jit(solution)/shard_map/reshape | solution.py:289
  12.0 0.7 %reshape.229.ms_ref = f32[32,224]{1,0:T(8,128)} reshape(f32[32,7,32]{2,1,0:T(8,128)S(1)} %broadcast_in_dim.145) | data formatting | bytes 57344 | tf_op jit(solution)/shard_map/reshape | solution.py:288
  12.7 39.0 %galerkin.1 = f32[24,7,1024]{2,1,0:T(8,128)} custom-call(s32[32]{0:T(128)} %reshape.227.sidx, s32[192]{0:T(256)} %reshape.228.wf, s32[32]{0:T(128)} %slot.1, s32[8]{0:T(128)} %broadcast_add_fusion.2.tinv, s32[8]{0:T(128)} %broadcast_add_fusion.1.pos, s32[24]{0:T(128)} %broadcast_add_fusion.cidx, bf16[32,7,192,192]{3,2,1,0:T(8,128)(2,1)} %a_ref.1, ...), custom_call_target="tpu_custom_call" | custom-call | tf_op jit(solution)/shard_map/galerkin/pallas_call | solution.py:328
  51.7 2.4 %copy.39 = f32[24,7,1024]{2,0,1:T(8,128)} copy(f32[24,7,1024]{2,1,0:T(8,128)} %galerkin.1) | data formatting | bytes 1376256 | tf_op jit(solution)/shard_map/galerkin/pallas_call | solution.py:328
  (29 shorter events, 1.2 us)

commit v2 on v1

--- a/solution.py
+++ b/solution.py
@@ -18,12 +18,131 @@
     return lax.broadcasted_iota(jnp.int32, shape, dim)
 
 
+def tables(
+    n_grp, n_dev, halo, group_rows, rows_own,
+    nbr, nbr_agg, slot, touch_agg, coarse_row,
+    tab, ms, ma,
+):
+    grp = lax.axis_index("grp")
+    dev = lax.axis_index("dev")
+    device = grp * n_dev + dev
+    faces, e_dev = nbr.shape
+    devices, touch = touch_agg.shape
+    wide = ms.shape[1]
+    width_c = wide // (faces + 1)
+
+    def where_sum(mask, value, axis):
+        return jnp.sum(jnp.where(mask, value, 0), axis=axis, keepdims=True)
+
+    def put(row, value):
+        tab[row:row + value.shape[0], 0:value.shape[1]] = value
+
+    near = [
+        jnp.where(grp > 0, device - n_dev, -2),
+        jnp.where(grp < n_grp - 1, device + n_dev, -2),
+        jnp.where(dev > 0, device - 1, -2),
+        jnp.where(dev < n_dev - 1, device + 1, -2),
+    ]
+    ids = nbr[...]
+    source = jnp.where(ids >= 0, jnp.maximum(ids, 0) // e_dev, -1)
+    local = ids - source * e_dev
+    hits = [jnp.max(jnp.where(source == n, 1.0, 0.0), axis=0, keepdims=True) for n in near]
+    below = jnp.where(iota((e_dev, e_dev), 0) < iota((e_dev, e_dev), 1), 1.0, 0.0).astype(BF16)
+    rank = jnp.dot(
+        jnp.concatenate(hits + hits, axis=0).astype(BF16), below, preferred_element_type=F32
+    ).astype(jnp.int32)
+    lanes = iota((halo, e_dev), 1)
+    for d in range(4):
+        found = (rank[d:d + 1] == iota((halo, e_dev), 0)) & (hits[d] > 0)
+        tab[8:8 + halo, d:d + 1] = where_sum(found, lanes, 1)
+    index = iota((e_dev, e_dev), 0)
+    where_from = [jnp.where(source[f:f + 1] == device, local[f:f + 1], 0) for f in range(faces)]
+    for d in range(4):
+        seen = jnp.zeros((e_dev, e_dev), jnp.int32)
+        for f in range(faces):
+            seen = jnp.where(ids[f:f + 1] == near[d] * e_dev + index, 1, seen)
+        seen = jnp.max(seen, axis=1, keepdims=True)
+        for f in range(faces):
+            ahead = where_sum(index < local[f:f + 1], seen, 0)
+            where_from[f] = jnp.where(
+                source[f:f + 1] == near[d], e_dev + d * halo + ahead, where_from[f]
+            )
+    for f in range(faces):
+        put(f, where_from[f])
+
+    row = iota((devices, 1), 0)
+    entries = touch_agg[...]
+    columns = [entries[:, t:t + 1] for t in range(touch)]
+    slots = slot[...]
+    put(19, slots)
+    own_agg = jnp.zeros((1, e_dev), jnp.int32)
+    for t in range(touch):
+        own_agg = jnp.where(slots == t, where_sum(row == device, columns[t], 0), own_agg)
+    valid = ids >= 0
+    same = valid & (nbr_agg[...] == own_agg)
+    apart = jnp.where(valid & jnp.logical_not(same), 1.0, 0.0).astype(BF16)
+    same = jnp.where(same, 1.0, 0.0).astype(BF16)
+    unit = jnp.where(iota((e_dev, e_dev), 0) == iota((e_dev, e_dev), 1), 1.0, 0.0).astype(BF16)
+    group = jnp.where(iota((faces, wide), 1) // width_c == iota((faces, wide), 0) + 1, 1.0, 0.0).astype(BF16)
+
+    def expand(flags):
+        turned = lax.dot_general(unit, flags, (((1,), (1,)), ((), ())), preferred_element_type=F32)
+        return jnp.dot(turned.astype(BF16), group, preferred_element_type=F32)
+
+    ms[...] = expand(same) + jnp.where(iota((e_dev, wide), 1) < width_c, 1.0, 0.0)
+    ma[...] = expand(apart)
+
+    n_agg = coarse_row.shape[1]
+    numbers = coarse_row[...]
+    across = iota((devices, n_agg), 1)
+    targets = [where_sum(columns[t] == across, numbers, 1) for t in range(touch)]
+    owners = [target // rows_own for target in targets]
+    lane = iota((devices, rows_own), 1)
+    present = jnp.zeros((devices, rows_own), F32)
+    for t in range(touch):
+        here = jnp.where(owners[t] == dev, targets[t] - owners[t] * rows_own, -1)
+        present = jnp.where(here == lane, 1.0, present)
+    mates = jnp.where(
+        iota((devices, devices), 0) // n_dev == iota((devices, devices), 1) // n_dev, 1.0, 0.0
+    ).astype(BF16)
+    shared = jnp.dot(mates, present.astype(BF16), preferred_element_type=F32) > 0
+    shared = jnp.where(shared, 1.0, 0.0)
+    lower = jnp.where(
+        iota((rows_own, rows_own), 0) < iota((rows_own, rows_own), 1), 1.0, 0.0
+    ).astype(BF16)
+    order = jnp.dot(shared.astype(BF16), lower, preferred_element_type=F32)
+    heads = where_sum(row % n_dev == 0, shared * (order + 1.0 + (row // n_dev * group_rows).astype(F32)), 0)
+    put(16, heads.astype(jnp.int32) - 1)
+    spots = jnp.sum(present * (order + 1.0), axis=1, keepdims=True).astype(jnp.int32) - 1
+    peer = iota((devices, n_dev), 1) + grp * n_dev
+    put(18, where_sum(peer == iota((devices, n_dev), 0), spots, 0))
+    inverse = jnp.full((1, n_dev), touch, jnp.int32)
+    for t in range(touch):
+        own = where_sum(row == device, owners[t], 0)
+        inverse = jnp.where(own == iota((1, n_dev), 1), t, inverse)
+    put(17, inverse)
+
+
+def finish(group_rows, tab, gathered, out_ref, flat):
+    rows_own, n_k, row_width = out_ref.shape
+    lane = 128
+    sub = row_width // lane
+
+    @pl.loop(0, rows_own)
+    def _(r):
+        at = tab[16, r]
+        safe = jnp.maximum(at, 0)
+        row = gathered[safe // group_rows, safe % group_rows].astype(F32)
+        flat[r] = jnp.where(at >= 0, row, 0.0)
+        for j in range(sub):
+            out_ref[r, :, j * lane:(j + 1) * lane] = flat[r, pl.ds(j, n_k, stride=sub), :]
+
+
 def kernel(
     n_grp, n_dev, halo, group_rows,
-    sidx, wf, slot, tinv, pos, cidx,
-    a_ref, p_ref, ms_ref, ma_ref,
-    out_ref,
-    a_buf, pool, pack, left, prod_s, prod_a, part_t, parts, inbox, gathered, flat,
+    tab, a_ref, p_ref, ms_ref, ma_ref,
+    gathered,
+    a_buf, pool, pack, left, prod_s, prod_a, part_t, parts, inbox,
     a_sem, h_send, h_recv, x_send, x_recv, g_send, g_recv,
 ):
     grp = lax.axis_index("grp")
@@ -31,7 +150,6 @@
     e_dev, width_c, width_b = p_ref.shape
     n_k = a_ref.shape[1]
     touch = part_t.shape[0] - 1
-    rows_own = out_ref.shape[0]
     wide = n_k * width_c
     lane = 128
     rep = lane // width_c
@@ -55,7 +173,7 @@
         )
 
     for j in range(4 * halo):
-        pack[j] = p_ref[sidx[j]]
+        pack[j] = p_ref[tab[8 + j % halo, j // halo]]
     pool[0:e_dev] = p_ref[...]
     pl.semaphore_wait(barrier, n_dev + n_grp - 2)
 
@@ -109,7 +227,7 @@
     @pl.loop(0, e_dev)
     def _(e):
         right = jnp.concatenate(
-            [pool[e]] + [pool[wf[e * (n_k - 1) + f]] for f in range(n_k - 1)], axis=0
+            [pool[e]] + [pool[tab[f, e]] for f in range(n_k - 1)], axis=0
         )
         full = lax.dot_general(
             left[e], right, (((1,), (1,)), ((), ())), preferred_element_type=F32
@@ -143,7 +261,7 @@
 
         def add(e, sums, t=t):
             sum_s, sum_a = sums
-            member = jnp.where(slot[e] == t, 1.0, 0.0).astype(F32)
+            member = jnp.where(tab[19, e] == t, 1.0, 0.0).astype(F32)
             return sum_s + prod_s[e] * member, sum_a + prod_a[e] * member
 
         sum_s, sum_a = lax.fori_loop(0, e_dev, add, (zero, zero), unroll=4)
@@ -154,7 +272,7 @@
         part_t[t] = rows.astype(BF16)
 
     for o in range(n_dev):
-        parts[o] = part_t[tinv[o]]
+        parts[o] = part_t[tab[17, o]]
     inbox[dev] = parts[dev]
 
     def part_copy(off):
@@ -187,7 +305,7 @@
     for j in range(group_rows):
         total = jnp.zeros(parts.shape[1:], F32)
         for d in range(n_dev):
-            member = jnp.where(pos[d] == j, 1.0, 0.0).astype(F32)
+            member = jnp.where(tab[18, d] == j, 1.0, 0.0).astype(F32)
             total = total + inbox[d].astype(F32) * member
         gathered[grp, j] = total.astype(BF16)
 
@@ -218,15 +336,6 @@
     for off in range(1, n_grp):
         row_arrival(off).wait_recv()
 
-    @pl.loop(0, rows_own)
-    def _(r):
-        at = cidx[r]
-        safe = jnp.maximum(at, 0)
-        row = gathered[safe // group_rows, safe % group_rows].astype(F32)
-        flat[r] = jnp.where(at >= 0, row, 0.0)
-        for j in range(sub):
-            out_ref[r, :, j * lane:(j + 1) * lane] = flat[r, pl.ds(j, n_k, stride=sub), :]
-
     for off in range(1, n_dev):
         part_copy(off).wait_send()
     for off in range(1, n_grp):
@@ -234,9 +343,6 @@
 
 
 def on_device(n_grp, n_dev, a_blocks, prolong_t, elem_slot, touch_agg, nbr, nbr_agg, coarse_row):
-    grp = lax.axis_index("grp")
-    dev = lax.axis_index("dev")
-    device = grp * n_dev + dev
     e_dev, width_c, width_b = prolong_t.shape
     n_k = a_blocks.shape[1]
     touch = touch_agg.shape[1]
@@ -246,89 +352,26 @@
     group_rows = (n_dev * half_y + 1 + half_y) // span_y
     rows_own = n_grp * group_rows
     assert touch <= n_dev
-    i32 = jnp.int32
-
-    def ar(n):
-        return jnp.arange(n, dtype=i32)
-
-    none = jnp.int32(-2)
-    near = jnp.stack([
-        jnp.where(grp > 0, device - n_dev, none),
-        jnp.where(grp < n_grp - 1, device + n_dev, none),
-        jnp.where(dev > 0, device - 1, none),
-        jnp.where(dev < n_dev - 1, device + 1, none),
-    ])
-    source = jnp.where(nbr >= 0, nbr // e_dev, -1)
-    local = nbr - source * e_dev
-    hit = jnp.any(source[None] == near[:, None, None], axis=2).astype(i32)
-    rank = jnp.sum(hit[:, None, :] * (ar(e_dev)[None, :] < ar(e_dev)[:, None]), axis=2)
-    sidx = jnp.sum(
-        jnp.where((rank[:, None, :] == ar(halo)[:, None]) & (hit[:, None, :] > 0), ar(e_dev), 0), axis=2
-    ).reshape(-1)
-    seen = jnp.any(
-        nbr[None, None] == (near[:, None] * e_dev + ar(e_dev))[:, :, None, None], axis=(2, 3)
-    ).astype(i32)
-    behind = jnp.sum(
-        jnp.where(
-            source[:, :, None, None] == near[:, None],
-            seen * (ar(e_dev) < local[:, :, None, None])
-            + jnp.where(ar(e_dev) == 0, (e_dev + ar(4) * halo)[:, None], 0),
-            0,
-        ),
-        axis=(2, 3),
-    )
-    wf = jnp.where(source == device, local, behind).reshape(-1)
-
-    touched = lax.dynamic_index_in_dim(touch_agg, device, 0, keepdims=False)
-    own_agg = jnp.sum(jnp.where(elem_slot[:, None] == ar(touch), touched, 0), axis=1)
-    valid = nbr >= 0
-    same = valid & (nbr_agg == own_agg[:, None])
-    apart = valid & jnp.logical_not(same)
-    true = jnp.ones((e_dev, 1), bool)
-    ms = jnp.repeat(jnp.concatenate([true, same], axis=1).astype(F32), width_c, axis=1)
-    ma = jnp.repeat(jnp.concatenate([~true, apart], axis=1).astype(F32), width_c, axis=1)
-
-    targets = jnp.sum(
-        jnp.where(touch_agg[:, :, None] == ar(coarse_row.shape[0]), coarse_row, 0), axis=2
-    )
-    owners = targets // rows_own
-    mine = owners == dev
-    place = jnp.where(mine, targets - owners * rows_own, -1)
-    present = jnp.any(
-        place.reshape(n_grp, n_dev * touch)[:, :, None] == ar(rows_own), axis=1
-    ).astype(i32)
-    cidx = jnp.sum(
-        present[:, :, None]
-        * (
-            present[:, None, :] * (ar(rows_own)[None, :] < ar(rows_own)[:, None])
-            + jnp.where(ar(rows_own) == 0, ar(n_grp)[:, None] * group_rows + 1, 0)[:, None, :]
-        ),
-        axis=(0, 2),
-    ) - 1
-    own_present = lax.dynamic_index_in_dim(present, grp, 0, keepdims=False)
-    group_place = lax.dynamic_slice_in_dim(place, grp * n_dev, n_dev, 0)
-    pos = jnp.sum(
-        jnp.where(
-            group_place[:, :, None] >= 0,
-            own_present * (ar(rows_own) < group_place[:, :, None]) + (ar(rows_own) == 0),
-            0,
-        ),
-        axis=(1, 2),
-    ) - 1
-    own_owner = lax.dynamic_index_in_dim(owners, device, 0, keepdims=False)
-    tinv = touch + jnp.sum(
-        jnp.where(own_owner[None, :] == ar(n_dev)[:, None], ar(touch) - touch, 0), axis=1
-    )
-
     lane = 128
     flat_rows = n_k * width_c * width_c // lane
     smem = pl.BlockSpec(memory_space=pltpu.SMEM)
     vmem = pl.BlockSpec(memory_space=pltpu.VMEM)
     wide = n_k * width_c
-    return pl.pallas_call(
+    tab, ms, ma = pl.pallas_call(
+        functools.partial(tables, n_grp, n_dev, halo, group_rows, rows_own),
+        out_shape=(
+            jax.ShapeDtypeStruct((24, lane), jnp.int32),
+            jax.ShapeDtypeStruct((e_dev, wide), F32),
+            jax.ShapeDtypeStruct((e_dev, wide), F32),
+        ),
+        in_specs=[vmem] * 5,
+        out_specs=(vmem, vmem, vmem),
+        name="index_tables",
+    )(nbr.T, nbr_agg.T, elem_slot.reshape(1, e_dev), touch_agg, coarse_row.reshape(1, -1))
+    gathered = pl.pallas_call(
         functools.partial(kernel, n_grp, n_dev, halo, group_rows),
-        out_shape=jax.ShapeDtypeStruct((rows_own, n_k, width_c * width_c), F32),
-        in_specs=[smem] * 6 + [pl.BlockSpec(memory_space=pl.ANY)] + [vmem] * 3,
+        out_shape=jax.ShapeDtypeStruct((n_grp, group_rows, flat_rows, lane), BF16),
+        in_specs=[smem, pl.BlockSpec(memory_space=pl.ANY)] + [vmem] * 3,
         out_specs=vmem,
         scratch_shapes=[
             pltpu.VMEM(a_blocks.shape, BF16),
@@ -340,8 +383,6 @@
             pltpu.VMEM((touch + 1, flat_rows, lane), BF16),
             pltpu.VMEM((n_dev, flat_rows, lane), BF16),
             pltpu.VMEM((n_dev, flat_rows, lane), BF16),
-            pltpu.VMEM((n_grp, group_rows, flat_rows, lane), BF16),
-            pltpu.VMEM((rows_own, flat_rows, lane), F32),
             pltpu.SemaphoreType.DMA((e_dev,)),
             pltpu.SemaphoreType.DMA((4,)),
             pltpu.SemaphoreType.DMA((4,)),
@@ -354,7 +395,15 @@
             collective_id=0, has_side_effects=True, vmem_limit_bytes=60 * 1024 * 1024
         ),
         name="galerkin",
-    )(sidx, wf, elem_slot, tinv, pos, cidx, a_blocks, prolong_t, ms, ma)
+    )(tab, a_blocks, prolong_t, ms, ma)
+    return pl.pallas_call(
+        functools.partial(finish, group_rows),
+        out_shape=jax.ShapeDtypeStruct((rows_own, n_k, width_c * width_c), F32),
+        in_specs=[smem, vmem],
+        out_specs=vmem,
+        scratch_shapes=[pltpu.VMEM((rows_own, flat_rows, lane), F32)],
+        name="index_finish",
+    )(tab, gathered)
 
 
 def solution(mesh):

time: 54.5 us -> 46.9 us (0.86)
  other arithmetic: 8.35 us -> 0 us
  Pallas kernels: 39 us -> 42.8 us
  local copies, waits for them, and re-layouts: 6.65 us -> 3.75 us
    pallas_call x0 -> x2, Pallas kernels: none -> 4.55 us  [the longest x1 2.58 us: on_device(): pl.pallas_call(functools.partial(finish, group_rows), out_shape=jax.Shape...]
    reduce_sum x8 -> x0, other arithmetic: 2.8 us -> none  [the longest x1 0.96 us: on_device(): jnp.sum(jnp.where(touch_agg[:, :, None] == ar(coarse_row.shape[0]), coars...]
    reshape x4 -> x0, local copies, waits for them, and re-layouts: 2.75 us -> none  [the longest x1 0.72 us: on_device(): jnp.repeat(jnp.concatenate([true, same], axis=1).astype(F32), width_c, ax...]
    sub x4 -> x0, other arithmetic: 1.79 us -> none  [the longest x1 0.7 us: on_device(): local = nbr - source * e_dev]
    unnamed x0 -> x1, local copies, waits for them, and re-layouts: none -> 1.37 us
    reduce_or x3 -> x0, other arithmetic: 1.16 us -> none  [the longest x1 0.93 us: on_device(): jnp.any(nbr[None, None] == (near[:, None] * e_dev + ar(e_dev))[:, :, None...]
    dynamic_slice x1 -> x0, local copies, waits for them, and re-layouts: 0.9 us -> none  [on_device(): touched = lax.dynamic_index_in_dim(touch_agg, device, 0, keepdims=False)]
    select_n x5 -> x0, other arithmetic: 0.88 us -> none  [the longest x1 0.7 us: on_device(): wf = jnp.where(source == device, local, behind).reshape(-1)]
where the time goes in v2:
time: 46.9 us; the launch traced here: 46.5 us
  Pallas kernels  42.8 us (91%)
  local copies, waits for them, and re-layouts  3.75 us (8%)
    pallas_call x1, Pallas kernels, on_device(): pl.pallas_call(functools.partial(kernel, n_grp, n_dev, halo, group_rows),...  38.2 us
    pallas_call x1, Pallas kernels, on_device(): pl.pallas_call(functools.partial(finish, group_rows), out_shape=jax.Shape...  2.58 us
    pallas_call x1, local copies, waits for them, and re-layouts, on_device(): pl.pallas_call(functools.partial(finish, group_rows), out_shape=jax.Shape...  2.38 us
    pallas_call x1, Pallas kernels, on_device(): pl.pallas_call(functools.partial(tables, n_grp, n_dev, halo, group_rows,...  1.96 us
    unnamed x1, local copies, waits for them, and re-layouts  1.37 us

profile of v2, /device:TPU:0, one launch (start us, length us, event | category | flops | bytes accessed | tf_op | source)
XLA Modules:
  0.0 46.5 jit_solution(6747512045492477636)
XLA Ops:
  0.0 1.4 %copy.8.touch_agg = s32[32,6]{1,0:T(8,128)} copy(s32[32,6]{0,1:T(8,128)} %param.10) | data formatting | bytes 1536 | tf_op args[3]
  1.4 2.0 %index_tables.1 = (s32[24,128]{1,0:T(8,128)}, f32[32,224]{1,0:T(8,128)}, f32[32,224]{1,0:T(8,128)}) custom-call(s32[6,32]{1,0:T(8,128)} %bitcast.4, s32[6,32]{1,0:T(8,128)} %bitcast.5, s32[1,32]{1,0:T(1,128)} %bitcast.7, s32[32,6]{1,0:T(8,128)} %copy.8.touch_agg, s32[1,136]{1,0:T(1,128)} %bitcast.6), custom_call_target="tpu_custom_call" | custom-call | tf_op jit(solution)/shard_map/index_tables/pallas_call | solution.py:360
  3.3 38.2 %galerkin.1.gathered = bf16[4,6,56,128]{3,2,1,0:T(8,128)(2,1)} custom-call(s32[24,128]{1,0:T(8,128)} %get-tuple-element.8.tab, bf16[32,7,192,192]{3,2,1,0:T(8,128)(2,1)} %a_ref.1, bf16[32,32,192]{2,1,0:T(8,128)(2,1)} %p_ref.1, f32[32,224]{1,0:T(8,128)} %get-tuple-element.9.ms_ref, f32[32,224]{1,0:T(8,128)} %get-tuple-element.10.ma_ref), custom_call_target="tpu_custom_call" | custom-call | tf_op jit(solution)/shard_map/galerkin/pallas_call | solution.py:371
  41.6 2.6 %index_finish.1 = f32[24,7,1024]{2,1,0:T(8,128)} custom-call(s32[24,128]{1,0:T(8,128)} %get-tuple-element.8.tab, bf16[4,6,56,128]{3,2,1,0:T(8,128)(2,1)} %galerkin.1.gathered), custom_call_target="tpu_custom_call" | custom-call | tf_op jit(solution)/shard_map/index_finish/pallas_call | solution.py:399
  44.2 2.4 %copy.9 = f32[24,7,1024]{2,0,1:T(8,128)} copy(f32[24,7,1024]{2,1,0:T(8,128)} %index_finish.1) | data formatting | bytes 1376256 | tf_op jit(solution)/shard_map/index_finish/pallas_call | solution.py:399

commit v3 on v2

--- a/solution.py
+++ b/solution.py
@@ -128,7 +128,7 @@
     lane = 128
     sub = row_width // lane
 
-    @pl.loop(0, rows_own)
+    @pl.loop(0, rows_own, unroll=4)
     def _(r):
         at = tab[16, r]
         safe = jnp.maximum(at, 0)
@@ -200,7 +200,7 @@
         def _(d=d, target=target):
             halo_copy(d, target).start()
 
-    @pl.loop(0, e_dev)
+    @pl.loop(0, e_dev, unroll=2)
     def _(e):
         a_copy(e).wait()
         own = p_ref[e]
@@ -224,7 +224,7 @@
 
     group_of_lane = iota((width_c, wide), 1) // width_c
 
-    @pl.loop(0, e_dev)
+    @pl.loop(0, e_dev, unroll=4)
     def _(e):
         right = jnp.concatenate(
             [pool[e]] + [pool[tab[f, e]] for f in range(n_k - 1)], axis=0
@@ -264,7 +264,7 @@
             member = jnp.where(tab[19, e] == t, 1.0, 0.0).astype(F32)
             return sum_s + prod_s[e] * member, sum_a + prod_a[e] * member
 
-        sum_s, sum_a = lax.fori_loop(0, e_dev, add, (zero, zero), unroll=4)
+        sum_s, sum_a = lax.fori_loop(0, e_dev, add, (zero, zero), unroll=8)
         both = jnp.concatenate([spread(sum_s, spread_s), spread(sum_a, spread_a)], axis=1)
         both = jnp.where(keep, both, 0.0).astype(BF16)
         rows = jnp.dot(squeeze, both, preferred_element_type=F32)

time: 46.9 us -> 41.9 us (0.89)
  Pallas kernels: 42.8 us -> 37.8 us
    pallas_call x1, Pallas kernels: 38.2 us -> 33.6 us  [on_device(): pl.pallas_call(functools.partial(kernel, n_grp, n_dev, halo, group_rows),...]
where the time goes in v3:
time: 41.9 us; the launch traced here: 41.6 us
  Pallas kernels  37.8 us (90%)
  local copies, waits for them, and re-layouts  3.75 us (9%)
    pallas_call x1, Pallas kernels, on_device(): pl.pallas_call(functools.partial(kernel, n_grp, n_dev, halo, group_rows),...  33.6 us
    pallas_call x1, local copies, waits for them, and re-layouts, on_device(): pl.pallas_call(functools.partial(finish, group_rows), out_shape=jax.Shape...  2.38 us
    pallas_call x1, Pallas kernels, on_device(): pl.pallas_call(functools.partial(finish, group_rows), out_shape=jax.Shape...  2.25 us
    pallas_call x1, Pallas kernels, on_device(): pl.pallas_call(functools.partial(tables, n_grp, n_dev, halo, group_rows,...  1.96 us
    unnamed x1, local copies, waits for them, and re-layouts  1.37 us

profile of v3, /device:TPU:0, one launch (start us, length us, event | category | flops | bytes accessed | tf_op | source)
XLA Modules:
  0.0 41.6 jit_solution(10188723357708375308)
XLA Ops:
  0.0 1.4 %copy.8.touch_agg = s32[32,6]{1,0:T(8,128)} copy(s32[32,6]{0,1:T(8,128)} %param.10) | data formatting | bytes 1536 | tf_op args[3]
  1.4 2.0 %index_tables.1 = (s32[24,128]{1,0:T(8,128)}, f32[32,224]{1,0:T(8,128)}, f32[32,224]{1,0:T(8,128)}) custom-call(s32[6,32]{1,0:T(8,128)} %bitcast.4, s32[6,32]{1,0:T(8,128)} %bitcast.5, s32[1,32]{1,0:T(1,128)} %bitcast.7, s32[32,6]{1,0:T(8,128)} %copy.8.touch_agg, s32[1,136]{1,0:T(1,128)} %bitcast.6), custom_call_target="tpu_custom_call" | custom-call | tf_op jit(solution)/shard_map/index_tables/pallas_call | solution.py:360
  3.3 33.6 %galerkin.1.gathered = bf16[4,6,56,128]{3,2,1,0:T(8,128)(2,1)} custom-call(s32[24,128]{1,0:T(8,128)} %get-tuple-element.8.tab, bf16[32,7,192,192]{3,2,1,0:T(8,128)(2,1)} %a_ref.1, bf16[32,32,192]{2,1,0:T(8,128)(2,1)} %p_ref.1, f32[32,224]{1,0:T(8,128)} %get-tuple-element.9.ms_ref, f32[32,224]{1,0:T(8,128)} %get-tuple-element.10.ma_ref), custom_call_target="tpu_custom_call" | custom-call | tf_op jit(solution)/shard_map/galerkin/pallas_call | solution.py:371
  37.0 2.2 %index_finish.1 = f32[24,7,1024]{2,1,0:T(8,128)} custom-call(s32[24,128]{1,0:T(8,128)} %get-tuple-element.8.tab, bf16[4,6,56,128]{3,2,1,0:T(8,128)(2,1)} %galerkin.1.gathered), custom_call_target="tpu_custom_call" | custom-call | tf_op jit(solution)/shard_map/index_finish/pallas_call | solution.py:399
  39.2 2.4 %copy.9 = f32[24,7,1024]{2,0,1:T(8,128)} copy(f32[24,7,1024]{2,1,0:T(8,128)} %index_finish.1) | data formatting | bytes 1376256 | tf_op jit(solution)/shard_map/index_finish/pallas_call | solution.py:399
